TPU v7x, 128 devices: a whole 4x4x4 slice. The times are simulated.
128 devices in a mesh: dp: 32 (over z, y, x_hi), section: 2 (over core), tensor: 2 (over x_lo).
Axes of the slice: x: 4 (x_hi: 2, x_lo: 2; x = x_hi * 2 + x_lo), y: 4, z: 4, core: 2. Of those that a mesh axis runs over, the one named last changes fastest.
Arguments:
- tokens: bfloat16 [512, 32, 1024], P('dp'), may hold values from -6 to 6
- counts: int32 [512], replicated, may hold values from 8 to 32, as said below
- assign: int32 [512], replicated, may hold values from 0 to 511, as said below
- qkv_weight: bfloat16 [2, 1024, 3, 1024], P('section', 'dp', None, 'tensor'), may hold values from -0.9375 to 0.9375
- out_weight: bfloat16 [2, 1024, 1024], P('section', 'dp'), may hold values from -0.1875 to 0.1875
- up_weight: bfloat16 [2, 1024, 4096], P('section', 'dp', 'tensor'), may hold values from -0.1875 to 0.1875
- up_bias: bfloat16 [2, 4096], P('section', 'tensor'), may hold values from -3 to 3
- down_weight: bfloat16 [2, 4096, 1024], P('section', 'tensor', 'dp'), may hold values from -0.09375 to 0.09375
- attn_gain: bfloat16 [2, 1024], P('section'), may hold values from 0.25 to 1.75
- mlp_gain: bfloat16 [2, 1024], P('section'), may hold values from 0.25 to 1.75
- final_gain: bfloat16 [1024], replicated, may hold values from 0.25 to 1.75
Outputs:
- encoded: bfloat16 [512, 32, 1024], P('dp', 'section', 'tensor')
Inputs may be any that keep to these rules, and one draw needn't show every extreme that they name: `counts`: every count is at least 8, and in every draw some image has all 32 slots live. assign is a permutation of the images. Slot j belongs to data group j // 16, so every data group receives 16 images; within one data group's slots the images stand in increasing order. Images of data group g are tokens rows g * 16 to (g + 1) * 16 - 1. No data group hands more than 1 images to one data group (itself included), and in every draw some pair of data groups exchanges exactly 1. Every data group receives some image from the data group half the axis away.
All inputs are finite; a program needn't handle non-finite values.
Results may differ from a plain program's by a relative error of at most 0.024.
The roundings to bfloat16 on the way count: a program that leaves them out, or rounds other values in their place, can miss the bound.
Values may be sent and summed in bfloat16 or wider, within the bound.
No kernel may reach another device: no remote copies, remote signals or barrier semaphores. Data moves between devices by JAX's collectives and lax.ppermute only.
A program may use at most 128 MiB of HBM per device.

v0:
```python
import jax
import jax.numpy as jnp
from jax import lax
from jax.sharding import PartitionSpec as P

MICRO = 4
HEAD_DIM = 64
epsilon = 1e-06


def cut_along(value, dim, size):
    lengths = value.shape
    tiles = value.reshape(*lengths[:dim], size, lengths[dim] // size, *lengths[dim + 1 :])
    return jnp.moveaxis(tiles, dim, 0)


def edges_of(length, count):
    unit = 8 if length >= 8 * count else 1
    return [length // unit * k // count * unit for k in range(1, count)]


def laid_out(tiles, dim):
    lengths = list(tiles.shape[1:])
    lengths[dim] *= tiles.shape[0]
    return jnp.moveaxis(tiles, 0, dim).reshape(lengths)


def cut_exchange(value, axis, pieces, split_dim, concat_dim):
    tiles = cut_along(value, split_dim, lax.axis_size(axis))
    widest = max(range(1, max(2, tiles.ndim - 1)), key=lambda d: tiles.shape[d])
    done = []
    for section in jnp.split(tiles, edges_of(tiles.shape[widest], pieces), axis=widest):
        if section.size:
            done.append(lax.all_to_all(section, axis, split_axis=0, concat_axis=0, tiled=True))
    return laid_out(jnp.concatenate(done, axis=widest), concat_dim)


def rows_first(arrays, axis, dims):
    turned = [jnp.moveaxis(a, dim, 0) for a, dim in zip(arrays, dims)]
    widths = [t[0].size for t in turned]
    both = jnp.concatenate([t.reshape(-1, w) for t, w in zip(turned, widths)], axis=1)
    out = lax.all_gather(both, axis, axis=0, tiled=True)
    tiles = jnp.split(out, [sum(widths[:k]) for k in range(1, len(widths))], axis=1)
    return tuple(
        (
            jnp.moveaxis(b.reshape(-1, *t.shape[1:]), 0, dim)
            for b, t, dim in zip(tiles, turned, dims)
        )
    )


def over_pieces(value, axis):
    return lax.all_gather(value, axis).astype(jnp.float32).sum(0)


def passed_along(value, axis, by):
    size = lax.axis_size(axis)
    return lax.ppermute(value, axis, [(i, (i + by) % size) for i in range(size)])


def from_root(value, axis, root):
    return lax.dynamic_index_in_dim(lax.all_gather(value, axis), root, 0, keepdims=False)


def layer_norm(values, gain_vector):
    average = jnp.mean(values, axis=-1, keepdims=True)
    centred = values - average
    spread = jnp.mean(centred * centred, axis=-1, keepdims=True)
    return centred * lax.rsqrt(spread + epsilon) * gain_vector.astype(jnp.float32)


def attend(normed, w_merged, live_count, head_dim):
    row_count = normed.shape[0]
    merged = jnp.dot(
        normed, w_merged.reshape(w_merged.shape[0], -1), preferred_element_type=jnp.float32
    )
    merged = merged.reshape(row_count, 3, -1, head_dim)
    scores = jnp.einsum(
        "qhd,khd->hqk", merged[:, 0], merged[:, 1], precision=lax.Precision.HIGHEST
    ) * head_dim ** (-0.5)
    visible = jnp.arange(row_count) < live_count
    scores = jnp.where(visible[None, None, :], scores, -1e30)
    weights = jax.nn.softmax(scores, axis=-1)
    mixed = jnp.einsum("hqk,khd->qhd", weights, merged[:, 2], precision=lax.Precision.HIGHEST)
    return mixed.reshape(row_count, -1).astype(jnp.bfloat16)


def local(
    tokens,
    counts,
    assign,
    qkv_weight,
    out_weight,
    up_weight,
    up_bias,
    down_weight,
    attn_gain,
    mlp_gain,
    final_gain,
):
    groups = lax.axis_size("dp")
    sections = lax.axis_size("section")
    tensor_ranks = lax.axis_size("tensor")
    images_dev, block_rows, model_width = tokens.shape
    quarter = model_width // tensor_ranks
    capacity = (images_dev + groups - 1) // groups
    total_images = assign.shape[0]
    batch_images = MICRO
    batch_count = images_dev // batch_images
    my_group = lax.axis_index("dp")
    my_section = lax.axis_index("section")
    tensor_index = lax.axis_index("tensor")
    numbers = jnp.arange(total_images, dtype=jnp.int32)
    matches = (assign[:, None] == numbers[None, :]).astype(jnp.int32)
    slot_of = jnp.sum(matches * numbers[:, None], axis=0)
    target = slot_of // images_dev
    source_group = numbers // images_dev
    earlier = (
        (source_group[:, None] == source_group[None, :])
        & (target[:, None] == target[None, :])
        & (numbers[None, :] < numbers[:, None])
    )
    rank_all = jnp.sum(earlier.astype(jnp.int32), axis=1)
    send_slot = lax.dynamic_slice_in_dim(
        target * capacity + rank_all, my_group * images_dev, images_dev
    )
    buffer_slots = jnp.arange(groups * capacity, dtype=jnp.int32)
    selector = (buffer_slots[:, None] == send_slot[None, :]).astype(jnp.bfloat16)
    outgoing = jnp.einsum(
        "sl,lbd->sbd", selector, tokens, preferred_element_type=jnp.float32
    ).astype(jnp.bfloat16)
    received = cut_exchange(outgoing, "dp", 2, 0, 0)
    my_images = lax.dynamic_slice_in_dim(assign, my_group * images_dev, images_dev)
    chosen = (my_images[:, None] == numbers[None, :]).astype(jnp.int32)
    receive_slot = jnp.sum(chosen * (source_group * capacity + rank_all)[None, :], axis=1)
    live_counts = jnp.sum(chosen * counts[None, :], axis=1)
    picker = (buffer_slots[None, :] == receive_slot[:, None]).astype(jnp.bfloat16)
    arrived = jnp.einsum(
        "js,sbd->jbd", picker, received, preferred_element_type=jnp.float32
    ).astype(jnp.bfloat16)
    arrived_batches = arrived.reshape(batch_count, batch_images, block_rows, model_width)
    live_batches = live_counts.reshape(batch_count, batch_images)
    qkv_full, out_full, up_full, down_full = rows_first(
        (qkv_weight, out_weight, up_weight, down_weight), "dp", (1, 1, 1, 2)
    )
    qkv_full = qkv_full[0]
    out_full = out_full[0]
    up_full = up_full[0]
    down_full = down_full[0]
    bias_row = up_bias[0].astype(jnp.float32)
    gain_attn = attn_gain[0]
    gain_mlp = mlp_gain[0]
    row_numbers = jnp.arange(block_rows)
    flat_rows = batch_images * block_rows

    def advance(step_index, state):
        carried, stored = state
        current = carried
        done_index = step_index - sections
        finishing = (my_section == 0) & (done_index >= 0)
        done_slot = jnp.clip(done_index, 0, batch_count - 1)
        finished_rows = row_numbers[None, :, None] < live_batches[done_slot][:, None, None]
        finished = jnp.where(
            finished_rows, layer_norm(current.astype(jnp.float32), final_gain), 0.0
        ).astype(jnp.bfloat16)
        stored = jnp.where(
            finishing, lax.dynamic_update_index_in_dim(stored, finished, done_slot, 0), stored
        )
        micro_index = step_index - my_section
        active = (micro_index >= 0) & (micro_index < batch_count)
        slot_index = jnp.clip(micro_index, 0, batch_count - 1)
        injected = lax.dynamic_index_in_dim(
            arrived_batches, jnp.clip(step_index, 0, batch_count - 1), 0, keepdims=False
        )
        incoming = jnp.where(my_section == 0, injected, current)
        live_now = live_batches[slot_index]

        def attention_part():
            normed = layer_norm(incoming.astype(jnp.float32), gain_attn).astype(jnp.bfloat16)
            return jax.vmap(
                lambda image_rows, live_count: attend(image_rows, qkv_full, live_count, HEAD_DIM)
            )(normed, live_now)

        def attention_spare():
            return jnp.zeros((batch_images, block_rows, quarter), jnp.bfloat16)

        head_out = lax.cond(active, attention_part, attention_spare)
        joined = lax.all_gather(head_out, "tensor", axis=2, tiled=True)

        def mlp_part():
            middle = incoming.reshape(flat_rows, model_width).astype(jnp.float32) + jnp.dot(
                joined.reshape(flat_rows, model_width), out_full, preferred_element_type=jnp.float32
            )
            normed_mlp = layer_norm(middle, gain_mlp).astype(jnp.bfloat16)
            hidden = jax.nn.gelu(
                jnp.dot(normed_mlp, up_full, preferred_element_type=jnp.float32) + bias_row,
                approximate=False,
            ).astype(jnp.bfloat16)
            return (middle, jnp.dot(hidden, down_full, preferred_element_type=jnp.float32))

        def mlp_spare():
            empty = jnp.zeros((flat_rows, model_width), jnp.float32)
            return (empty, empty)

        middle, partial_value = lax.cond(active, mlp_part, mlp_spare)
        summed = over_pieces(partial_value.astype(jnp.bfloat16), "tensor").astype(jnp.float32)
        updated = (
            (middle + summed).astype(jnp.bfloat16).reshape(batch_images, block_rows, model_width)
        )
        carried = passed_along(updated, "section", 1)
        return (carried, stored)

    initial = (
        jnp.zeros((batch_images, block_rows, model_width), jnp.bfloat16),
        jnp.zeros((batch_count, batch_images, block_rows, model_width), jnp.bfloat16),
    )
    carried, stored = lax.fori_loop(0, batch_count + sections, advance, initial)
    stored = stored.reshape(images_dev, block_rows, model_width)
    my_piece = lax.dynamic_slice_in_dim(stored, tensor_index * quarter, quarter, 2)
    spread = from_root(my_piece, "section", 0)
    section_rows = block_rows // sections
    return lax.dynamic_slice_in_dim(spread, my_section * section_rows, section_rows, 1)


def solution(mesh):
    in_specs = (
        P("dp", None, None),
        P(),
        P(),
        P("section", "dp", None, "tensor"),
        P("section", "dp", None),
        P("section", "dp", "tensor"),
        P("section", "tensor"),
        P("section", "tensor", "dp"),
        P("section", None),
        P("section", None),
        P(),
    )
    out_specs = P("dp", "section", "tensor")
    return jax.shard_map(local, mesh=mesh, in_specs=in_specs, out_specs=out_specs, check_vma=False)
```

profile of v0, /device:TPU:1, one launch (start us, length us, event | category | flops | bytes accessed | tf_op | source)
XLA Modules:
  0.0 434.2 jit_solution(15417628559894977373)
XLA Ops:
  7.6 1.8 pad_maximum_fusion
  13.5 11.3 %all-to-all-start = ((bf16[32,1,16,1024]{3,2,1,0:T(8,128)(2,1)}), bf16[32,1,16,1024]{3,2,1,0:T(8,128)(2,1)S(1)}, u32[]{:S(2)}, u32[]{:S(2)}) async-start(bf16[32,1,16,1024]{3,2,1,0:T(8,128)(2,1)} %copy.71), calls=%async_computation | async-start | bytes 2097152 | tf_op jit(solution)/shard_map/all_to_all | solution.py:34
  26.4 20.6 %all-to-all-done = bf16[32,1,16,1024]{3,2,1,0:T(8,128)(2,1)S(1)} async-done(((bf16[32,1,16,1024]{3,2,1,0:T(8,128)(2,1)}), bf16[32,1,16,1024]{3,2,1,0:T(8,128)(2,1)S(1)}, u32[]{:S(2)}, u32[]{:S(2)}) %all-to-all-start) | async-done | bytes 1048608 | tf_op jit(solution)/shard_map/all_to_all | solution.py:34
  47.0 4.0 all-to-all-start.1
  53.7 20.1 %all-to-all-done.1 = bf16[32,1,16,1024]{3,2,1,0:T(8,128)(2,1)S(1)} async-done(((bf16[32,1,16,1024]{3,2,1,0:T(8,128)(2,1)}), bf16[32,1,16,1024]{3,2,1,0:T(8,128)(2,1)S(1)}, u32[]{:S(2)}, u32[]{:S(2)}) %all-to-all-start.1) | async-done | bytes 1048608 | tf_op jit(solution)/shard_map/all_to_all | solution.py:34
  77.7 87.1 %all-gather.8.cloned.1.call-done = bf16[1024,6656]{1,0:T(8,128)(2,1)} async-done(((bf16[32,6656]{1,0:T(8,128)(2,1)}), bf16[1024,6656]{1,0:T(8,128)(2,1)}) %all-gather.8.cloned.1.call-update) | async-done | bytes 13631504 | tf_op jit(solution)/shard_map/all_gather | solution.py:42
  164.7 6.1 %slice_bitcast_fusion = (bf16[2048,1024]{0,1:T(8,128)(2,1)}, bf16[1024,2048]{1,0:T(8,128)(2,1)}) fusion(bf16[1024,6656]{1,0:T(8,128)(2,1)} %all-gather.8.cloned.1.call-done), kind=kLoop, calls=%fused_computation.138 | loop fusion | bytes 16777216 | tf_op jit(solution)/shard_map/squeeze | solution.py:149
  170.8 6.4 %copy.77 = bf16[2048,1024]{1,0:T(8,128)(2,1)} copy(bf16[2048,1024]{0,1:T(8,128)(2,1)} %get-tuple-element.580) | data formatting | bytes 8388608
  177.2 3.7 split.26
  181.0 3.2 split.27
  185.3 228.6 %while.18 = (s32[]{:T(128)}, bf16[4,32,1024]{2,1,0:T(8,128)(2,1)S(1)}, bf16[4,4,32,1024]{3,2,1,0:T(8,128)(2,1)}, s32[]{:T(128)}, pred[]{:T(512)}, /*index=5*/bf1...) while((s32[]{:T(128)}, ...), condition=%wide.region_18.19_spmd.clone, body=%wide.region_4.18_spmd.clone.sunk | while | flops 1818134144 | bytes 30876236 | solution.py:217
  186.3 4.5 %all_gather.44 = bf16[4,32,1024]{2,1,0:T(8,128)(2,1)S(1)} all-gather(bf16[4,32,512]{2,1,0:T(8,128)(2,1)S(1)} %get-tuple-element.747), channel_id=1, replica_groups=mesh['dp'=32,'section'=2,'tensor'=2] {'tensor'}, dimensions={2}, use_global_device_ids=true | all-gather | bytes 393216 | tf_op jit(solution)/shard_map/while/body/eval_jaxpr/all_gather | solution.py:188
  191.8 5.9 %all-gather.4 = bf16[256,1024]{1,0:T(8,128)(2,1)S(1)} all-gather(bf16[128,1024]{1,0:T(8,128)(2,1)S(1)} %convert_element_type.215), channel_id=2, replica_groups=mesh['dp'=32,'section'=2,'tensor'=2] {'tensor'}, dimensions={0}, use_global_device_ids=true | all-gather | bytes 786432 | tf_op jit(solution)/shard_map/while/body/eval_jaxpr/all_gather | solution.py:53
  198.9 25.8 %collective-permute-start = (bf16[4,32,1024]{2,1,0:T(8,128)(2,1)S(1)}, bf16[4,32,1024]{2,1,0:T(8,128)(2,1)S(1)}, u32[]{:S(2)}, u32[]{:S(2)}) collective-permute-start(bf16[4,32,1024]{2,1,0:T(8,128)(2,1)S(1)} %bitcast.86), channel_id=1, source_target_pairs={{0,2},{2,0},{1,3},{3,1},{4,6},{6,4},{5,7},{7,5},{8,10},{10,8},{9,1... | collective-permute-start | bytes 786440 | tf_op jit(solution)/shard_map/while/body/eval_jaxpr/ppermute | solution.py:58
  225.1 1.9 fusion.139
  228.1 11.5 %conditional.6 = (bf16[4,32,512]{2,1,0:T(8,128)(2,1)S(1)}) conditional(s32[]{:T(128)} %convert_element_type.214, () %tuple.78, (bf16[4,32,1024]{2,1,0:T(8,128)(2,1)S(1)}, bf16[1024]{0:T(1024)(128)(2,1)S(1)}, bf16[1024,1536]{1,0:T(8,128)(2,1)}, s32[]{:T(128)}, s32[4,4]{1,0:T(4,128)S(1)}) %tuple.79), branch_computations={%region_5.5_spmd, %region_6.10_spmd} | conditional | flops 454720768 | bytes 9734996 | solution.py:187
  228.5 3.5 fusion.2
  234.8 2.3 fusion.127
  237.2 2.1 fusion.5
  239.6 5.7 %all_gather.44 = bf16[4,32,1024]{2,1,0:T(8,128)(2,1)S(1)} all-gather(bf16[4,32,512]{2,1,0:T(8,128)(2,1)S(1)} %get-tuple-element.747), channel_id=1, replica_groups=mesh['dp'=32,'section'=2,'tensor'=2] {'tensor'}, dimensions={2}, use_global_device_ids=true | all-gather | bytes 393216 | tf_op jit(solution)/shard_map/while/body/eval_jaxpr/all_gather | solution.py:188
  245.3 11.4 %conditional.7 = (f32[128,1024]{1,0:T(8,128)}, f32[128,1024]{1,0:T(8,128)S(1)}) conditional(s32[]{:T(128)} %convert_element_type.214, () %tuple.77, (bf16[4,32,1024]{2,1,0:T(8,128)(2,1)S(1)}, bf16[4,32,1024]{2,1,0:T(8,128)(2,1)S(1)}, bf16[1024,1024]{1,0:T(8,128)(2,1)}, bf16[1024]{0:T(1024)(128)(2,1)S(1)}, bf16[1024,2048]{1,0:T(8,128)(2,1)}, ...), branch_computations={%region_11.11_spmd, %region_12.14_spmd} | conditional | flops 1360790656 | bytes 13130256 | solution.py:205
  245.3 2.9 fusion.128
  249.4 7.3 %fusion.29 = f32[128,1024]{1,0:T(8,128)S(1)} fusion(bf16[2048,1024]{1,0:T(8,128)(2,1)} %get-tuple-element.410, bf16[1024,2048]{1,0:T(8,128)(2,1)} %get-tuple-element.408, f32[2048]{0:T(1024)S(1)} %get-tuple-element.409, f32[128,1024]{1,0:T(8,128)} %get-tuple-element.685, f32[1024]{0:T(1024)S(1)} %convert_element_type.116, f32[128]{0:T(128)S(1)} %add_rsqrt_fusion.1, ...), kind=kOutput, calls=%fused_computation.50 | convolution fusion | flops 1091567616 | bytes 9450496 | tf_op jit(solution)/shard_map/while/body/eval_jaxpr/cond/branch_1_fun/dot_general | solution.py:199
  256.8 7.6 %all-gather.4 = bf16[256,1024]{1,0:T(8,128)(2,1)S(1)} all-gather(bf16[128,1024]{1,0:T(8,128)(2,1)S(1)} %convert_element_type.215), channel_id=2, replica_groups=mesh['dp'=32,'section'=2,'tensor'=2] {'tensor'}, dimensions={0}, use_global_device_ids=true | all-gather | bytes 786432 | tf_op jit(solution)/shard_map/while/body/eval_jaxpr/all_gather | solution.py:53
  265.7 1.8 collective-permute-start
  267.9 1.9 fusion.139
  270.9 11.5 %conditional.6 = (bf16[4,32,512]{2,1,0:T(8,128)(2,1)S(1)}) conditional(s32[]{:T(128)} %convert_element_type.214, () %tuple.78, (bf16[4,32,1024]{2,1,0:T(8,128)(2,1)S(1)}, bf16[1024]{0:T(1024)(128)(2,1)S(1)}, bf16[1024,1536]{1,0:T(8,128)(2,1)}, s32[]{:T(128)}, s32[4,4]{1,0:T(4,128)S(1)}) %tuple.79), branch_computations={%region_5.5_spmd, %region_6.10_spmd} | conditional | flops 454720768 | bytes 9734996 | solution.py:187
  271.3 3.5 fusion.2
  277.6 2.3 fusion.127
  280.0 2.1 fusion.5
  282.4 5.7 %all_gather.44 = bf16[4,32,1024]{2,1,0:T(8,128)(2,1)S(1)} all-gather(bf16[4,32,512]{2,1,0:T(8,128)(2,1)S(1)} %get-tuple-element.747), channel_id=1, replica_groups=mesh['dp'=32,'section'=2,'tensor'=2] {'tensor'}, dimensions={2}, use_global_device_ids=true | all-gather | bytes 393216 | tf_op jit(solution)/shard_map/while/body/eval_jaxpr/all_gather | solution.py:188
  288.1 11.4 %conditional.7 = (f32[128,1024]{1,0:T(8,128)}, f32[128,1024]{1,0:T(8,128)S(1)}) conditional(s32[]{:T(128)} %convert_element_type.214, () %tuple.77, (bf16[4,32,1024]{2,1,0:T(8,128)(2,1)S(1)}, bf16[4,32,1024]{2,1,0:T(8,128)(2,1)S(1)}, bf16[1024,1024]{1,0:T(8,128)(2,1)}, bf16[1024]{0:T(1024)(128)(2,1)S(1)}, bf16[1024,2048]{1,0:T(8,128)(2,1)}, ...), branch_computations={%region_11.11_spmd, %region_12.14_spmd} | conditional | flops 1360790656 | bytes 13130256 | solution.py:205
  288.1 2.9 fusion.128
  292.2 7.3 %fusion.29 = f32[128,1024]{1,0:T(8,128)S(1)} fusion(bf16[2048,1024]{1,0:T(8,128)(2,1)} %get-tuple-element.410, bf16[1024,2048]{1,0:T(8,128)(2,1)} %get-tuple-element.408, f32[2048]{0:T(1024)S(1)} %get-tuple-element.409, f32[128,1024]{1,0:T(8,128)} %get-tuple-element.685, f32[1024]{0:T(1024)S(1)} %convert_element_type.116, f32[128]{0:T(128)S(1)} %add_rsqrt_fusion.1, ...), kind=kOutput, calls=%fused_computation.50 | convolution fusion | flops 1091567616 | bytes 9450496 | tf_op jit(solution)/shard_map/while/body/eval_jaxpr/cond/branch_1_fun/dot_general | solution.py:199
  299.6 7.6 %all-gather.4 = bf16[256,1024]{1,0:T(8,128)(2,1)S(1)} all-gather(bf16[128,1024]{1,0:T(8,128)(2,1)S(1)} %convert_element_type.215), channel_id=2, replica_groups=mesh['dp'=32,'section'=2,'tensor'=2] {'tensor'}, dimensions={0}, use_global_device_ids=true | all-gather | bytes 786432 | tf_op jit(solution)/shard_map/while/body/eval_jaxpr/all_gather | solution.py:53
  308.5 1.8 collective-permute-start
  310.7 1.9 fusion.139
  313.7 11.5 %conditional.6 = (bf16[4,32,512]{2,1,0:T(8,128)(2,1)S(1)}) conditional(s32[]{:T(128)} %convert_element_type.214, () %tuple.78, (bf16[4,32,1024]{2,1,0:T(8,128)(2,1)S(1)}, bf16[1024]{0:T(1024)(128)(2,1)S(1)}, bf16[1024,1536]{1,0:T(8,128)(2,1)}, s32[]{:T(128)}, s32[4,4]{1,0:T(4,128)S(1)}) %tuple.79), branch_computations={%region_5.5_spmd, %region_6.10_spmd} | conditional | flops 454720768 | bytes 9734996 | solution.py:187
  314.1 3.5 fusion.2
  320.4 2.3 fusion.127
  322.8 2.1 fusion.5
  325.2 5.7 %all_gather.44 = bf16[4,32,1024]{2,1,0:T(8,128)(2,1)S(1)} all-gather(bf16[4,32,512]{2,1,0:T(8,128)(2,1)S(1)} %get-tuple-element.747), channel_id=1, replica_groups=mesh['dp'=32,'section'=2,'tensor'=2] {'tensor'}, dimensions={2}, use_global_device_ids=true | all-gather | bytes 393216 | tf_op jit(solution)/shard_map/while/body/eval_jaxpr/all_gather | solution.py:188
  330.9 11.4 %conditional.7 = (f32[128,1024]{1,0:T(8,128)}, f32[128,1024]{1,0:T(8,128)S(1)}) conditional(s32[]{:T(128)} %convert_element_type.214, () %tuple.77, (bf16[4,32,1024]{2,1,0:T(8,128)(2,1)S(1)}, bf16[4,32,1024]{2,1,0:T(8,128)(2,1)S(1)}, bf16[1024,1024]{1,0:T(8,128)(2,1)}, bf16[1024]{0:T(1024)(128)(2,1)S(1)}, bf16[1024,2048]{1,0:T(8,128)(2,1)}, ...), branch_computations={%region_11.11_spmd, %region_12.14_spmd} | conditional | flops 1360790656 | bytes 13130256 | solution.py:205
  330.9 2.9 fusion.128
  335.0 7.3 %fusion.29 = f32[128,1024]{1,0:T(8,128)S(1)} fusion(bf16[2048,1024]{1,0:T(8,128)(2,1)} %get-tuple-element.410, bf16[1024,2048]{1,0:T(8,128)(2,1)} %get-tuple-element.408, f32[2048]{0:T(1024)S(1)} %get-tuple-element.409, f32[128,1024]{1,0:T(8,128)} %get-tuple-element.685, f32[1024]{0:T(1024)S(1)} %convert_element_type.116, f32[128]{0:T(128)S(1)} %add_rsqrt_fusion.1, ...), kind=kOutput, calls=%fused_computation.50 | convolution fusion | flops 1091567616 | bytes 9450496 | tf_op jit(solution)/shard_map/while/body/eval_jaxpr/cond/branch_1_fun/dot_general | solution.py:199
  342.4 7.6 %all-gather.4 = bf16[256,1024]{1,0:T(8,128)(2,1)S(1)} all-gather(bf16[128,1024]{1,0:T(8,128)(2,1)S(1)} %convert_element_type.215), channel_id=2, replica_groups=mesh['dp'=32,'section'=2,'tensor'=2] {'tensor'}, dimensions={0}, use_global_device_ids=true | all-gather | bytes 786432 | tf_op jit(solution)/shard_map/while/body/eval_jaxpr/all_gather | solution.py:53
  351.3 1.8 collective-permute-start
  353.5 1.9 fusion.139
  356.5 11.5 %conditional.6 = (bf16[4,32,512]{2,1,0:T(8,128)(2,1)S(1)}) conditional(s32[]{:T(128)} %convert_element_type.214, () %tuple.78, (bf16[4,32,1024]{2,1,0:T(8,128)(2,1)S(1)}, bf16[1024]{0:T(1024)(128)(2,1)S(1)}, bf16[1024,1536]{1,0:T(8,128)(2,1)}, s32[]{:T(128)}, s32[4,4]{1,0:T(4,128)S(1)}) %tuple.79), branch_computations={%region_5.5_spmd, %region_6.10_spmd} | conditional | flops 454720768 | bytes 9734996 | solution.py:187
  356.9 3.5 fusion.2
  363.2 2.3 fusion.127
  365.6 2.1 fusion.5
  368.0 4.5 %all_gather.44 = bf16[4,32,1024]{2,1,0:T(8,128)(2,1)S(1)} all-gather(bf16[4,32,512]{2,1,0:T(8,128)(2,1)S(1)} %get-tuple-element.747), channel_id=1, replica_groups=mesh['dp'=32,'section'=2,'tensor'=2] {'tensor'}, dimensions={2}, use_global_device_ids=true | all-gather | bytes 393216 | tf_op jit(solution)/shard_map/while/body/eval_jaxpr/all_gather | solution.py:188
  372.5 11.4 %conditional.7 = (f32[128,1024]{1,0:T(8,128)}, f32[128,1024]{1,0:T(8,128)S(1)}) conditional(s32[]{:T(128)} %convert_element_type.214, () %tuple.77, (bf16[4,32,1024]{2,1,0:T(8,128)(2,1)S(1)}, bf16[4,32,1024]{2,1,0:T(8,128)(2,1)S(1)}, bf16[1024,1024]{1,0:T(8,128)(2,1)}, bf16[1024]{0:T(1024)(128)(2,1)S(1)}, bf16[1024,2048]{1,0:T(8,128)(2,1)}, ...), branch_computations={%region_11.11_spmd, %region_12.14_spmd} | conditional | flops 1360790656 | bytes 13130256 | solution.py:205
  372.5 2.9 fusion.128
  376.6 7.3 %fusion.29 = f32[128,1024]{1,0:T(8,128)S(1)} fusion(bf16[2048,1024]{1,0:T(8,128)(2,1)} %get-tuple-element.410, bf16[1024,2048]{1,0:T(8,128)(2,1)} %get-tuple-element.408, f32[2048]{0:T(1024)S(1)} %get-tuple-element.409, f32[128,1024]{1,0:T(8,128)} %get-tuple-element.685, f32[1024]{0:T(1024)S(1)} %convert_element_type.116, f32[128]{0:T(128)S(1)} %add_rsqrt_fusion.1, ...), kind=kOutput, calls=%fused_computation.50 | convolution fusion | flops 1091567616 | bytes 9450496 | tf_op jit(solution)/shard_map/while/body/eval_jaxpr/cond/branch_1_fun/dot_general | solution.py:199
  384.0 5.9 %all-gather.4 = bf16[256,1024]{1,0:T(8,128)(2,1)S(1)} all-gather(bf16[128,1024]{1,0:T(8,128)(2,1)S(1)} %convert_element_type.215), channel_id=2, replica_groups=mesh['dp'=32,'section'=2,'tensor'=2] {'tensor'}, dimensions={0}, use_global_device_ids=true | all-gather | bytes 786432 | tf_op jit(solution)/shard_map/while/body/eval_jaxpr/all_gather | solution.py:53
  391.6 1.9 fusion.139
  394.6 5.2 %all_gather.44 = bf16[4,32,1024]{2,1,0:T(8,128)(2,1)S(1)} all-gather(bf16[4,32,512]{2,1,0:T(8,128)(2,1)S(1)} %get-tuple-element.747), channel_id=1, replica_groups=mesh['dp'=32,'section'=2,'tensor'=2] {'tensor'}, dimensions={2}, use_global_device_ids=true | all-gather | bytes 393216 | tf_op jit(solution)/shard_map/while/body/eval_jaxpr/all_gather | solution.py:188
  400.8 7.2 %all-gather.4 = bf16[256,1024]{1,0:T(8,128)(2,1)S(1)} all-gather(bf16[128,1024]{1,0:T(8,128)(2,1)S(1)} %convert_element_type.215), channel_id=2, replica_groups=mesh['dp'=32,'section'=2,'tensor'=2] {'tensor'}, dimensions={0}, use_global_device_ids=true | all-gather | bytes 786432 | tf_op jit(solution)/shard_map/while/body/eval_jaxpr/all_gather | solution.py:53
  409.2 2.3 collective-permute-start
  412.0 1.9 fusion.139
  413.9 1.9 constant_dynamic-slice_fusion.1
  415.9 9.7 %all-gather.10.cloned.1.call-done = bf16[32,32,512]{2,1,0:T(8,128)(2,1)} async-done(((bf16[16,32,512]{2,1,0:T(8,128)(2,1)}), bf16[32,32,512]{2,1,0:T(8,128)(2,1)}) %all-gather.10.cloned.1.call-update) | async-done | bytes 1048592 | tf_op jit(solution)/shard_map/all_gather | solution.py:62
  (194 shorter events, 55.5 us)
Async XLA Ops:
  6.5 4.2 copy-start
  6.5 158.2 %all-gather.8.cloned.1.call-start = ((), (), s32[]{:S(2)}) async-start(), calls=%async_computation.2 | async-start | bytes 14057472 | tf_op jit(solution)/shard_map/all_gather | solution.py:42
  11.9 39.9 %copy-start.5 = (s32[512]{0:T(512)S(1)}, s32[512]{0:T(512)}, u32[]{:S(2)}) copy-start(s32[512]{0:T(512)} %param.18) | copy-start | bytes 6148
  11.9 40.2 %copy-start.2 = (bf16[1,2048]{1,0:T(2,128)(2,1)S(1)}, bf16[1,2048]{1,0:T(2,128)(2,1)}, u32[]{:S(2)}) copy-start(bf16[1,2048]{1,0:T(2,128)(2,1)} %param.23) | copy-start | bytes 12292
  11.9 40.2 %copy-start.3 = (bf16[1,1024]{1,0:T(2,128)(2,1)S(1)}, bf16[1,1024]{1,0:T(2,128)(2,1)}, u32[]{:S(2)}) copy-start(bf16[1,1024]{1,0:T(2,128)(2,1)} %param.25) | copy-start | bytes 6148
  12.0 40.2 %copy-start.4 = (bf16[1,1024]{1,0:T(2,128)(2,1)S(1)}, bf16[1,1024]{1,0:T(2,128)(2,1)}, u32[]{:S(2)}) copy-start(bf16[1,1024]{1,0:T(2,128)(2,1)} %param.26) | copy-start | bytes 6148
  13.5 33.5 %all-to-all-start = ((bf16[32,1,16,1024]{3,2,1,0:T(8,128)(2,1)}), bf16[32,1,16,1024]{3,2,1,0:T(8,128)(2,1)S(1)}, u32[]{:S(2)}, u32[]{:S(2)}) async-start(bf16[32,1,16,1024]{3,2,1,0:T(8,128)(2,1)} %copy.71), calls=%async_computation | async-start | bytes 2097152 | tf_op jit(solution)/shard_map/all_to_all | solution.py:34
  47.0 26.8 %all-to-all-start.1 = ((bf16[32,1,16,1024]{3,2,1,0:T(8,128)(2,1)}), bf16[32,1,16,1024]{3,2,1,0:T(8,128)(2,1)S(1)}, u32[]{:S(2)}, u32[]{:S(2)}) async-start(bf16[32,1,16,1024]{3,2,1,0:T(8,128)(2,1)} %copy.72), calls=%async_computation.1 | async-start | bytes 2097152 | tf_op jit(solution)/shard_map/all_to_all | solution.py:34
  51.0 374.6 %all-gather.10.cloned.1.call-start = ((), (), s32[]{:S(2)}) async-start(), calls=%async_computation.3 | async-start | bytes 1572864 | tf_op jit(solution)/shard_map/all_gather | solution.py:62
  181.0 4.3 copy-start.1
  198.9 28.2 %collective-permute-start = (bf16[4,32,1024]{2,1,0:T(8,128)(2,1)S(1)}, bf16[4,32,1024]{2,1,0:T(8,128)(2,1)S(1)}, u32[]{:S(2)}, u32[]{:S(2)}) collective-permute-start(bf16[4,32,1024]{2,1,0:T(8,128)(2,1)S(1)} %bitcast.86), channel_id=1, source_target_pairs={{0,2},{2,0},{1,3},{3,1},{4,6},{6,4},{5,7},{7,5},{8,10},{10,8},{9,1... | collective-permute-start | bytes 786440 | tf_op jit(solution)/shard_map/while/body/eval_jaxpr/ppermute | solution.py:58
  265.7 4.2 collective-permute-start
  308.5 4.2 collective-permute-start
  351.3 4.2 collective-permute-start
  391.1 2.5 collective-permute-start
  409.2 4.7 %collective-permute-start = (bf16[4,32,1024]{2,1,0:T(8,128)(2,1)S(1)}, bf16[4,32,1024]{2,1,0:T(8,128)(2,1)S(1)}, u32[]{:S(2)}, u32[]{:S(2)}) collective-permute-start(bf16[4,32,1024]{2,1,0:T(8,128)(2,1)S(1)} %bitcast.86), channel_id=1, source_target_pairs={{0,2},{2,0},{1,3},{3,1},{4,6},{6,4},{5,7},{7,5},{8,10},{10,8},{9,1... | collective-permute-start | bytes 786440 | tf_op jit(solution)/shard_map/while/body/eval_jaxpr/ppermute | solution.py:58
Sparse Core Ops, SparseCore 0:
  10.5 154.2 all-gather.7
  416.0 9.5 all-gather.9
where the time goes:
time: 437 us; the launch traced here: 434 us
  waiting for transfers between devices  137 us (31%)
  matrix products  74.6 us (17%)
  blocking collectives  73.2 us (17%)
  starting transfers between devices  49 us (11%)
  local copies, waits for them, and re-layouts  47.6 us (11%)
  other arithmetic  37.8 us (9%)
  between operations  13.6 us (3%)
    all_gather x1, waiting for transfers between devices, rows_first(): out = lax.all_gather(both, axis, axis=0, tiled=True)  87.1 us
    all_gather x6, blocking collectives, over_pieces(): return lax.all_gather(value, axis).astype(jnp.float32).sum(0)  41.9 us
    all_to_all x2, waiting for transfers between devices, cut_exchange(): lax.all_to_all(section, axis, split_axis=0, concat_axis=0, tiled=True)  40.7 us
    ppermute x6, starting transfers between devices, passed_along(): lax.ppermute(value, axis, [(i, (i + by) % size) for i in range(size)])  33.6 us
    all_gather x6, blocking collectives, advance(): joined = lax.all_gather(head_out, 'tensor', axis=2, tiled=True)  31.3 us
    dot_general x4, matrix products, mlp_part(): jnp.dot(hidden, down_full, preferred_element_type=jnp.float32)  29.2 us
    all_to_all x2, starting transfers between devices, cut_exchange(): lax.all_to_all(section, axis, split_axis=0, concat_axis=0, tiled=True)  15.3 us
    dot_general x4, matrix products, attend(): jnp.dot(normed, w_merged.reshape(w_merged.shape[0], -1), preferred_elemen...  13.8 us
  transfers between devices with their start and end apart: 10, of which 4 were waited for; matrix products, arithmetic and copies ran while one was open for 6% of the time, Pallas kernels for 0%

commit v1 on v0

--- a/solution.py
+++ b/solution.py
@@ -185,7 +185,7 @@
             return jnp.zeros((batch_images, block_rows, quarter), jnp.bfloat16)
 
         head_out = lax.cond(active, attention_part, attention_spare)
-        joined = lax.all_gather(head_out, "tensor", axis=2, tiled=True)
+        joined = jnp.concatenate(lax.all_gather(head_out, "tensor"), axis=2)
 
         def mlp_part():
             middle = incoming.reshape(flat_rows, model_width).astype(jnp.float32) + jnp.dot(

time: 437 us -> 438 us (level)
  no operation moved by 1% of the time
where the time goes in v1:
time: 438 us; the launch traced here: 436 us
  waiting for transfers between devices  137 us (31%)
  matrix products  74.7 us (17%)
  blocking collectives  73.2 us (17%)
  starting transfers between devices  49.3 us (11%)
  local copies, waits for them, and re-layouts  48.9 us (11%)
  other arithmetic  37.8 us (9%)
  between operations  13.6 us (3%)
    all_gather x1, waiting for transfers between devices, rows_first(): out = lax.all_gather(both, axis, axis=0, tiled=True)  87.1 us
    all_gather x6, blocking collectives, over_pieces(): return lax.all_gather(value, axis).astype(jnp.float32).sum(0)  41.9 us
    all_to_all x2, waiting for transfers between devices, cut_exchange(): lax.all_to_all(section, axis, split_axis=0, concat_axis=0, tiled=True)  40.7 us
    ppermute x6, starting transfers between devices, passed_along(): lax.ppermute(value, axis, [(i, (i + by) % size) for i in range(size)])  33.9 us
    all_gather x6, blocking collectives, advance(): joined = jnp.concatenate(lax.all_gather(head_out, 'tensor'), axis=2)  31.3 us
    dot_general x4, matrix products, mlp_part(): jnp.dot(hidden, down_full, preferred_element_type=jnp.float32)  29.2 us
    all_to_all x2, starting transfers between devices, cut_exchange(): lax.all_to_all(section, axis, split_axis=0, concat_axis=0, tiled=True)  15.3 us
    dot_general x4, matrix products, attend(): jnp.dot(normed, w_merged.reshape(w_merged.shape[0], -1), preferred_elemen...  13.8 us
  transfers between devices with their start and end apart: 10, of which 4 were waited for; matrix products, arithmetic and copies ran while one was open for 6% of the time, Pallas kernels for 0%

profile of v1, /device:TPU:1, one launch (start us, length us, event | category | flops | bytes accessed | tf_op | source)
XLA Modules:
  0.0 435.8 jit_solution(5650916842259438520)
XLA Ops:
  7.6 1.8 pad_maximum_fusion
  13.5 11.3 %all-to-all-start = ((bf16[32,1,16,1024]{3,2,1,0:T(8,128)(2,1)}), bf16[32,1,16,1024]{3,2,1,0:T(8,128)(2,1)S(1)}, u32[]{:S(2)}, u32[]{:S(2)}) async-start(bf16[32,1,16,1024]{3,2,1,0:T(8,128)(2,1)} %copy.75), calls=%async_computation | async-start | bytes 2097152 | tf_op jit(solution)/shard_map/all_to_all | solution.py:34
  26.4 20.6 %all-to-all-done = bf16[32,1,16,1024]{3,2,1,0:T(8,128)(2,1)S(1)} async-done(((bf16[32,1,16,1024]{3,2,1,0:T(8,128)(2,1)}), bf16[32,1,16,1024]{3,2,1,0:T(8,128)(2,1)S(1)}, u32[]{:S(2)}, u32[]{:S(2)}) %all-to-all-start) | async-done | bytes 1048608 | tf_op jit(solution)/shard_map/all_to_all | solution.py:34
  47.0 4.0 all-to-all-start.1
  53.7 20.1 %all-to-all-done.1 = bf16[32,1,16,1024]{3,2,1,0:T(8,128)(2,1)S(1)} async-done(((bf16[32,1,16,1024]{3,2,1,0:T(8,128)(2,1)}), bf16[32,1,16,1024]{3,2,1,0:T(8,128)(2,1)S(1)}, u32[]{:S(2)}, u32[]{:S(2)}) %all-to-all-start.1) | async-done | bytes 1048608 | tf_op jit(solution)/shard_map/all_to_all | solution.py:34
  77.7 87.1 %all-gather.12.cloned.1.call-done = bf16[1024,6656]{1,0:T(8,128)(2,1)} async-done(((bf16[32,6656]{1,0:T(8,128)(2,1)}), bf16[1024,6656]{1,0:T(8,128)(2,1)}) %all-gather.12.cloned.1.call-update) | async-done | bytes 13631504 | tf_op jit(solution)/shard_map/all_gather | solution.py:42
  164.7 6.1 %slice_bitcast_fusion = (bf16[2048,1024]{0,1:T(8,128)(2,1)}, bf16[1024,2048]{1,0:T(8,128)(2,1)}) fusion(bf16[1024,6656]{1,0:T(8,128)(2,1)} %all-gather.12.cloned.1.call-done), kind=kLoop, calls=%fused_computation.138 | loop fusion | bytes 16777216 | tf_op jit(solution)/shard_map/squeeze | solution.py:149
  170.8 6.4 %copy.81 = bf16[2048,1024]{1,0:T(8,128)(2,1)} copy(bf16[2048,1024]{0,1:T(8,128)(2,1)} %get-tuple-element.608) | data formatting | bytes 8388608
  177.2 3.7 split.26
  181.0 3.2 split.27
  185.3 230.2 %while.18 = (s32[]{:T(128)}, bf16[4,32,1024]{2,1,0:T(8,128)(2,1)S(1)}, bf16[4,4,32,1024]{3,2,1,0:T(8,128)(2,1)}, s32[]{:T(128)}, pred[]{:T(512)}, /*index=5*/bf1...) while((s32[]{:T(128)}, ...), condition=%wide.region_18.19_spmd.clone, body=%wide.region_4.18_spmd.clone.sunk | while | flops 1818134144 | bytes 31924812 | solution.py:217
  186.3 4.5 %all-gather.7 = bf16[8,32,512]{2,1,0:T(8,128)(2,1)S(1)} all-gather(bf16[4,32,512]{2,1,0:T(8,128)(2,1)S(1)} %get-tuple-element.775), channel_id=2, replica_groups=mesh['dp'=32,'section'=2,'tensor'=2] {'tensor'}, dimensions={0}, use_global_device_ids=true | all-gather | bytes 393216 | tf_op jit(solution)/shard_map/while/body/eval_jaxpr/all_gather | solution.py:188
  191.8 5.9 %all-gather.8 = bf16[256,1024]{1,0:T(8,128)(2,1)S(1)} all-gather(bf16[128,1024]{1,0:T(8,128)(2,1)S(1)} %convert_element_type.215), channel_id=3, replica_groups=mesh['dp'=32,'section'=2,'tensor'=2] {'tensor'}, dimensions={0}, use_global_device_ids=true | all-gather | bytes 786432 | tf_op jit(solution)/shard_map/while/body/eval_jaxpr/all_gather | solution.py:53
  198.9 26.1 %collective-permute-start = (bf16[4,32,1024]{2,1,0:T(8,128)(2,1)S(1)}, bf16[4,32,1024]{2,1,0:T(8,128)(2,1)S(1)}, u32[]{:S(2)}, u32[]{:S(2)}) collective-permute-start(bf16[4,32,1024]{2,1,0:T(8,128)(2,1)S(1)} %bitcast.95), channel_id=1, source_target_pairs={{0,2},{2,0},{1,3},{3,1},{4,6},{6,4},{5,7},{7,5},{8,10},{10,8},{9,1... | collective-permute-start | bytes 786440 | tf_op jit(solution)/shard_map/while/body/eval_jaxpr/ppermute | solution.py:58
  225.5 1.9 fusion.139
  228.4 11.5 %conditional.6 = (bf16[4,32,512]{2,1,0:T(8,128)(2,1)S(1)}) conditional(s32[]{:T(128)} %convert_element_type.214, () %tuple.82, (bf16[4,32,1024]{2,1,0:T(8,128)(2,1)S(1)}, bf16[1024]{0:T(1024)(128)(2,1)S(1)}, bf16[1024,1536]{1,0:T(8,128)(2,1)}, s32[]{:T(128)}, s32[4,4]{1,0:T(4,128)S(1)}) %tuple.83), branch_computations={%region_5.5_spmd, %region_6.10_spmd} | conditional | flops 454720768 | bytes 9734996 | solution.py:187
  228.8 3.5 fusion.2
  235.1 2.3 fusion.127
  237.5 2.1 fusion.5
  239.9 5.7 %all-gather.7 = bf16[8,32,512]{2,1,0:T(8,128)(2,1)S(1)} all-gather(bf16[4,32,512]{2,1,0:T(8,128)(2,1)S(1)} %get-tuple-element.775), channel_id=2, replica_groups=mesh['dp'=32,'section'=2,'tensor'=2] {'tensor'}, dimensions={0}, use_global_device_ids=true | all-gather | bytes 393216 | tf_op jit(solution)/shard_map/while/body/eval_jaxpr/all_gather | solution.py:188
  245.6 11.7 %conditional.7 = (f32[128,1024]{1,0:T(8,128)}, f32[128,1024]{1,0:T(8,128)S(1)}) conditional(s32[]{:T(128)} %convert_element_type.214, () %tuple.81, (bf16[4,32,1024]{2,1,0:T(8,128)(2,1)S(1)}, bf16[4,32,2,512]{3,1,0,2:T(8,128)(2,1)S(1)}, bf16[1024,1024]{1,0:T(8,128)(2,1)}, bf16[1024]{0:T(1024)(128)(2,1)S(1)}, bf16[1024,2048]{1,0:T(8,128)(2,1)}, ...), branch_computations={%region_11.11_spmd, %region_12.14_spmd} | conditional | flops 1360790656 | bytes 14178832 | solution.py:205
  245.9 2.9 fusion.128
  250.1 7.3 %fusion.29 = f32[128,1024]{1,0:T(8,128)S(1)} fusion(bf16[2048,1024]{1,0:T(8,128)(2,1)} %get-tuple-element.410, bf16[1024,2048]{1,0:T(8,128)(2,1)} %get-tuple-element.408, f32[2048]{0:T(1024)S(1)} %get-tuple-element.409, f32[128,1024]{1,0:T(8,128)} %get-tuple-element.713, f32[1024]{0:T(1024)S(1)} %convert_element_type.116, f32[128]{0:T(128)S(1)} %add_rsqrt_fusion.1, ...), kind=kOutput, calls=%fused_computation.50 | convolution fusion | flops 1091567616 | bytes 9450496 | tf_op jit(solution)/shard_map/while/body/eval_jaxpr/cond/branch_1_fun/dot_general | solution.py:199
  257.4 7.6 %all-gather.8 = bf16[256,1024]{1,0:T(8,128)(2,1)S(1)} all-gather(bf16[128,1024]{1,0:T(8,128)(2,1)S(1)} %convert_element_type.215), channel_id=3, replica_groups=mesh['dp'=32,'section'=2,'tensor'=2] {'tensor'}, dimensions={0}, use_global_device_ids=true | all-gather | bytes 786432 | tf_op jit(solution)/shard_map/while/body/eval_jaxpr/all_gather | solution.py:53
  266.3 1.8 collective-permute-start
  268.6 1.9 fusion.139
  271.5 11.5 %conditional.6 = (bf16[4,32,512]{2,1,0:T(8,128)(2,1)S(1)}) conditional(s32[]{:T(128)} %convert_element_type.214, () %tuple.82, (bf16[4,32,1024]{2,1,0:T(8,128)(2,1)S(1)}, bf16[1024]{0:T(1024)(128)(2,1)S(1)}, bf16[1024,1536]{1,0:T(8,128)(2,1)}, s32[]{:T(128)}, s32[4,4]{1,0:T(4,128)S(1)}) %tuple.83), branch_computations={%region_5.5_spmd, %region_6.10_spmd} | conditional | flops 454720768 | bytes 9734996 | solution.py:187
  271.9 3.5 fusion.2
  278.2 2.3 fusion.127
  280.6 2.1 fusion.5
  283.1 5.7 %all-gather.7 = bf16[8,32,512]{2,1,0:T(8,128)(2,1)S(1)} all-gather(bf16[4,32,512]{2,1,0:T(8,128)(2,1)S(1)} %get-tuple-element.775), channel_id=2, replica_groups=mesh['dp'=32,'section'=2,'tensor'=2] {'tensor'}, dimensions={0}, use_global_device_ids=true | all-gather | bytes 393216 | tf_op jit(solution)/shard_map/while/body/eval_jaxpr/all_gather | solution.py:188
  288.7 11.8 %conditional.7 = (f32[128,1024]{1,0:T(8,128)}, f32[128,1024]{1,0:T(8,128)S(1)}) conditional(s32[]{:T(128)} %convert_element_type.214, () %tuple.81, (bf16[4,32,1024]{2,1,0:T(8,128)(2,1)S(1)}, bf16[4,32,2,512]{3,1,0,2:T(8,128)(2,1)S(1)}, bf16[1024,1024]{1,0:T(8,128)(2,1)}, bf16[1024]{0:T(1024)(128)(2,1)S(1)}, bf16[1024,2048]{1,0:T(8,128)(2,1)}, ...), branch_computations={%region_11.11_spmd, %region_12.14_spmd} | conditional | flops 1360790656 | bytes 14178832 | solution.py:205
  289.1 2.9 fusion.128
  293.2 7.3 %fusion.29 = f32[128,1024]{1,0:T(8,128)S(1)} fusion(bf16[2048,1024]{1,0:T(8,128)(2,1)} %get-tuple-element.410, bf16[1024,2048]{1,0:T(8,128)(2,1)} %get-tuple-element.408, f32[2048]{0:T(1024)S(1)} %get-tuple-element.409, f32[128,1024]{1,0:T(8,128)} %get-tuple-element.713, f32[1024]{0:T(1024)S(1)} %convert_element_type.116, f32[128]{0:T(128)S(1)} %add_rsqrt_fusion.1, ...), kind=kOutput, calls=%fused_computation.50 | convolution fusion | flops 1091567616 | bytes 9450496 | tf_op jit(solution)/shard_map/while/body/eval_jaxpr/cond/branch_1_fun/dot_general | solution.py:199
  300.5 7.6 %all-gather.8 = bf16[256,1024]{1,0:T(8,128)(2,1)S(1)} all-gather(bf16[128,1024]{1,0:T(8,128)(2,1)S(1)} %convert_element_type.215), channel_id=3, replica_groups=mesh['dp'=32,'section'=2,'tensor'=2] {'tensor'}, dimensions={0}, use_global_device_ids=true | all-gather | bytes 786432 | tf_op jit(solution)/shard_map/while/body/eval_jaxpr/all_gather | solution.py:53
  309.4 1.8 collective-permute-start
  311.7 1.9 fusion.139
  314.6 11.5 %conditional.6 = (bf16[4,32,512]{2,1,0:T(8,128)(2,1)S(1)}) conditional(s32[]{:T(128)} %convert_element_type.214, () %tuple.82, (bf16[4,32,1024]{2,1,0:T(8,128)(2,1)S(1)}, bf16[1024]{0:T(1024)(128)(2,1)S(1)}, bf16[1024,1536]{1,0:T(8,128)(2,1)}, s32[]{:T(128)}, s32[4,4]{1,0:T(4,128)S(1)}) %tuple.83), branch_computations={%region_5.5_spmd, %region_6.10_spmd} | conditional | flops 454720768 | bytes 9734996 | solution.py:187
  315.0 3.5 fusion.2
  321.3 2.3 fusion.127
  323.8 2.1 fusion.5
  326.2 5.7 %all-gather.7 = bf16[8,32,512]{2,1,0:T(8,128)(2,1)S(1)} all-gather(bf16[4,32,512]{2,1,0:T(8,128)(2,1)S(1)} %get-tuple-element.775), channel_id=2, replica_groups=mesh['dp'=32,'section'=2,'tensor'=2] {'tensor'}, dimensions={0}, use_global_device_ids=true | all-gather | bytes 393216 | tf_op jit(solution)/shard_map/while/body/eval_jaxpr/all_gather | solution.py:188
  331.9 11.7 %conditional.7 = (f32[128,1024]{1,0:T(8,128)}, f32[128,1024]{1,0:T(8,128)S(1)}) conditional(s32[]{:T(128)} %convert_element_type.214, () %tuple.81, (bf16[4,32,1024]{2,1,0:T(8,128)(2,1)S(1)}, bf16[4,32,2,512]{3,1,0,2:T(8,128)(2,1)S(1)}, bf16[1024,1024]{1,0:T(8,128)(2,1)}, bf16[1024]{0:T(1024)(128)(2,1)S(1)}, bf16[1024,2048]{1,0:T(8,128)(2,1)}, ...), branch_computations={%region_11.11_spmd, %region_12.14_spmd} | conditional | flops 1360790656 | bytes 14178832 | solution.py:205
  332.2 2.9 fusion.128
  336.3 7.3 %fusion.29 = f32[128,1024]{1,0:T(8,128)S(1)} fusion(bf16[2048,1024]{1,0:T(8,128)(2,1)} %get-tuple-element.410, bf16[1024,2048]{1,0:T(8,128)(2,1)} %get-tuple-element.408, f32[2048]{0:T(1024)S(1)} %get-tuple-element.409, f32[128,1024]{1,0:T(8,128)} %get-tuple-element.713, f32[1024]{0:T(1024)S(1)} %convert_element_type.116, f32[128]{0:T(128)S(1)} %add_rsqrt_fusion.1, ...), kind=kOutput, calls=%fused_computation.50 | convolution fusion | flops 1091567616 | bytes 9450496 | tf_op jit(solution)/shard_map/while/body/eval_jaxpr/cond/branch_1_fun/dot_general | solution.py:199
  343.7 7.6 %all-gather.8 = bf16[256,1024]{1,0:T(8,128)(2,1)S(1)} all-gather(bf16[128,1024]{1,0:T(8,128)(2,1)S(1)} %convert_element_type.215), channel_id=3, replica_groups=mesh['dp'=32,'section'=2,'tensor'=2] {'tensor'}, dimensions={0}, use_global_device_ids=true | all-gather | bytes 786432 | tf_op jit(solution)/shard_map/while/body/eval_jaxpr/all_gather | solution.py:53
  352.5 1.8 collective-permute-start
  354.8 1.9 fusion.139
  357.8 11.5 %conditional.6 = (bf16[4,32,512]{2,1,0:T(8,128)(2,1)S(1)}) conditional(s32[]{:T(128)} %convert_element_type.214, () %tuple.82, (bf16[4,32,1024]{2,1,0:T(8,128)(2,1)S(1)}, bf16[1024]{0:T(1024)(128)(2,1)S(1)}, bf16[1024,1536]{1,0:T(8,128)(2,1)}, s32[]{:T(128)}, s32[4,4]{1,0:T(4,128)S(1)}) %tuple.83), branch_computations={%region_5.5_spmd, %region_6.10_spmd} | conditional | flops 454720768 | bytes 9734996 | solution.py:187
  358.1 3.5 fusion.2
  364.4 2.3 fusion.127
  366.9 2.1 fusion.5
  369.3 4.5 %all-gather.7 = bf16[8,32,512]{2,1,0:T(8,128)(2,1)S(1)} all-gather(bf16[4,32,512]{2,1,0:T(8,128)(2,1)S(1)} %get-tuple-element.775), channel_id=2, replica_groups=mesh['dp'=32,'section'=2,'tensor'=2] {'tensor'}, dimensions={0}, use_global_device_ids=true | all-gather | bytes 393216 | tf_op jit(solution)/shard_map/while/body/eval_jaxpr/all_gather | solution.py:188
  373.8 11.7 %conditional.7 = (f32[128,1024]{1,0:T(8,128)}, f32[128,1024]{1,0:T(8,128)S(1)}) conditional(s32[]{:T(128)} %convert_element_type.214, () %tuple.81, (bf16[4,32,1024]{2,1,0:T(8,128)(2,1)S(1)}, bf16[4,32,2,512]{3,1,0,2:T(8,128)(2,1)S(1)}, bf16[1024,1024]{1,0:T(8,128)(2,1)}, bf16[1024]{0:T(1024)(128)(2,1)S(1)}, bf16[1024,2048]{1,0:T(8,128)(2,1)}, ...), branch_computations={%region_11.11_spmd, %region_12.14_spmd} | conditional | flops 1360790656 | bytes 14178832 | solution.py:205
  374.1 2.9 fusion.128
  378.2 7.3 %fusion.29 = f32[128,1024]{1,0:T(8,128)S(1)} fusion(bf16[2048,1024]{1,0:T(8,128)(2,1)} %get-tuple-element.410, bf16[1024,2048]{1,0:T(8,128)(2,1)} %get-tuple-element.408, f32[2048]{0:T(1024)S(1)} %get-tuple-element.409, f32[128,1024]{1,0:T(8,128)} %get-tuple-element.713, f32[1024]{0:T(1024)S(1)} %convert_element_type.116, f32[128]{0:T(128)S(1)} %add_rsqrt_fusion.1, ...), kind=kOutput, calls=%fused_computation.50 | convolution fusion | flops 1091567616 | bytes 9450496 | tf_op jit(solution)/shard_map/while/body/eval_jaxpr/cond/branch_1_fun/dot_general | solution.py:199
  385.6 5.9 %all-gather.8 = bf16[256,1024]{1,0:T(8,128)(2,1)S(1)} all-gather(bf16[128,1024]{1,0:T(8,128)(2,1)S(1)} %convert_element_type.215), channel_id=3, replica_groups=mesh['dp'=32,'section'=2,'tensor'=2] {'tensor'}, dimensions={0}, use_global_device_ids=true | all-gather | bytes 786432 | tf_op jit(solution)/shard_map/while/body/eval_jaxpr/all_gather | solution.py:53
  393.2 1.9 fusion.139
  396.2 5.2 %all-gather.7 = bf16[8,32,512]{2,1,0:T(8,128)(2,1)S(1)} all-gather(bf16[4,32,512]{2,1,0:T(8,128)(2,1)S(1)} %get-tuple-element.775), channel_id=2, replica_groups=mesh['dp'=32,'section'=2,'tensor'=2] {'tensor'}, dimensions={0}, use_global_device_ids=true | all-gather | bytes 393216 | tf_op jit(solution)/shard_map/while/body/eval_jaxpr/all_gather | solution.py:188
  402.4 7.2 %all-gather.8 = bf16[256,1024]{1,0:T(8,128)(2,1)S(1)} all-gather(bf16[128,1024]{1,0:T(8,128)(2,1)S(1)} %convert_element_type.215), channel_id=3, replica_groups=mesh['dp'=32,'section'=2,'tensor'=2] {'tensor'}, dimensions={0}, use_global_device_ids=true | all-gather | bytes 786432 | tf_op jit(solution)/shard_map/while/body/eval_jaxpr/all_gather | solution.py:53
  410.8 2.3 collective-permute-start
  413.5 1.9 fusion.139
  415.5 1.9 constant_dynamic-slice_fusion.1
  417.5 9.7 %all-gather.14.cloned.1.call-done = bf16[32,32,512]{2,1,0:T(8,128)(2,1)} async-done(((bf16[16,32,512]{2,1,0:T(8,128)(2,1)}), bf16[32,32,512]{2,1,0:T(8,128)(2,1)}) %all-gather.14.cloned.1.call-update) | async-done | bytes 1048592 | tf_op jit(solution)/shard_map/all_gather | solution.py:62
  (202 shorter events, 56.8 us)
Async XLA Ops:
  6.5 4.2 copy-start
  6.5 158.2 %all-gather.12.cloned.1.call-start = ((), (), s32[]{:S(2)}) async-start(), calls=%async_computation.2 | async-start | bytes 14057472 | tf_op jit(solution)/shard_map/all_gather | solution.py:42
  11.9 39.9 %copy-start.5 = (s32[512]{0:T(512)S(1)}, s32[512]{0:T(512)}, u32[]{:S(2)}) copy-start(s32[512]{0:T(512)} %param.18) | copy-start | bytes 6148
  11.9 40.2 %copy-start.2 = (bf16[1,2048]{1,0:T(2,128)(2,1)S(1)}, bf16[1,2048]{1,0:T(2,128)(2,1)}, u32[]{:S(2)}) copy-start(bf16[1,2048]{1,0:T(2,128)(2,1)} %param.23) | copy-start | bytes 12292
  11.9 40.2 %copy-start.3 = (bf16[1,1024]{1,0:T(2,128)(2,1)S(1)}, bf16[1,1024]{1,0:T(2,128)(2,1)}, u32[]{:S(2)}) copy-start(bf16[1,1024]{1,0:T(2,128)(2,1)} %param.25) | copy-start | bytes 6148
  12.0 40.2 %copy-start.4 = (bf16[1,1024]{1,0:T(2,128)(2,1)S(1)}, bf16[1,1024]{1,0:T(2,128)(2,1)}, u32[]{:S(2)}) copy-start(bf16[1,1024]{1,0:T(2,128)(2,1)} %param.26) | copy-start | bytes 6148
  13.5 33.5 %all-to-all-start = ((bf16[32,1,16,1024]{3,2,1,0:T(8,128)(2,1)}), bf16[32,1,16,1024]{3,2,1,0:T(8,128)(2,1)S(1)}, u32[]{:S(2)}, u32[]{:S(2)}) async-start(bf16[32,1,16,1024]{3,2,1,0:T(8,128)(2,1)} %copy.75), calls=%async_computation | async-start | bytes 2097152 | tf_op jit(solution)/shard_map/all_to_all | solution.py:34
  47.0 26.8 %all-to-all-start.1 = ((bf16[32,1,16,1024]{3,2,1,0:T(8,128)(2,1)}), bf16[32,1,16,1024]{3,2,1,0:T(8,128)(2,1)S(1)}, u32[]{:S(2)}, u32[]{:S(2)}) async-start(bf16[32,1,16,1024]{3,2,1,0:T(8,128)(2,1)} %copy.76), calls=%async_computation.1 | async-start | bytes 2097152 | tf_op jit(solution)/shard_map/all_to_all | solution.py:34
  51.0 376.2 %all-gather.14.cloned.1.call-start = ((), (), s32[]{:S(2)}) async-start(), calls=%async_computation.3 | async-start | bytes 1572864 | tf_op jit(solution)/shard_map/all_gather | solution.py:62
  181.0 4.3 copy-start.1
  198.9 28.5 %collective-permute-start = (bf16[4,32,1024]{2,1,0:T(8,128)(2,1)S(1)}, bf16[4,32,1024]{2,1,0:T(8,128)(2,1)S(1)}, u32[]{:S(2)}, u32[]{:S(2)}) collective-permute-start(bf16[4,32,1024]{2,1,0:T(8,128)(2,1)S(1)} %bitcast.95), channel_id=1, source_target_pairs={{0,2},{2,0},{1,3},{3,1},{4,6},{6,4},{5,7},{7,5},{8,10},{10,8},{9,1... | collective-permute-start | bytes 786440 | tf_op jit(solution)/shard_map/while/body/eval_jaxpr/ppermute | solution.py:58
  266.3 4.2 collective-permute-start
  309.4 4.2 collective-permute-start
  352.5 4.2 collective-permute-start
  392.7 2.5 collective-permute-start
  410.8 4.7 %collective-permute-start = (bf16[4,32,1024]{2,1,0:T(8,128)(2,1)S(1)}, bf16[4,32,1024]{2,1,0:T(8,128)(2,1)S(1)}, u32[]{:S(2)}, u32[]{:S(2)}) collective-permute-start(bf16[4,32,1024]{2,1,0:T(8,128)(2,1)S(1)} %bitcast.95), channel_id=1, source_target_pairs={{0,2},{2,0},{1,3},{3,1},{4,6},{6,4},{5,7},{7,5},{8,10},{10,8},{9,1... | collective-permute-start | bytes 786440 | tf_op jit(solution)/shard_map/while/body/eval_jaxpr/ppermute | solution.py:58
Sparse Core Ops, SparseCore 0:
  10.5 154.2 all-gather.11
  417.6 9.5 all-gather.13
